TPU v7x, 32 devices: a whole 2x2x4 slice. The times are simulated.
32 devices in a mesh: pipe: 1, seq: 32 (over z, y, x, core).
Axes of the slice: x: 2, y: 2, z: 4, core: 2. Of those that a mesh axis runs over, the one named last changes fastest.
Arguments:
- previous: bfloat16 [1, 4096, 8192], P('pipe', 'seq'), may hold values from -6 to 6
- saved_head_inputs: bfloat16 [1, 4096, 8192], P('pipe', 'seq'), may hold values from -0.29882812 to 0.29882812
- input_b: bfloat16 [1, 4096, 1024], P('pipe', 'seq'), may hold values from -0.5 to 0.5
- input_c: bfloat16 [1, 4096, 1024], P('pipe', 'seq'), may hold values from -0.5 to 0.5
- steps: float32 [1, 4096, 128], P('pipe', 'seq'), may hold values from 0.1 to 6553.6, as said below
- decay_rate: float32 [1, 128], P('pipe'), may hold values from 6.1035156e-05 to 0.05
- skip_gain: float32 [1, 128], P('pipe'), may hold values from 0.5 to 1.5
- segment_ids: int32 [1, 4096], P('pipe', 'seq'), may hold values from 0 to 3, never falling along the last dimension, each value on 1 to 2048 neighbouring positions
- advantage_mask: int32 [4096], P('seq'), may hold values 0 or 1
Outputs:
- grad_x: bfloat16 [1, 4096, 8192], P('pipe', 'seq')
- grad_b: bfloat16 [1, 4096, 1024], P('pipe', 'seq')
- grad_c: bfloat16 [1, 4096, 1024], P('pipe', 'seq')
- bypass_gain_adjoint: float32 [1, 128], P('pipe')
Inputs may be any that keep to these rules, and one draw needn't show every extreme that they name: `steps`: Positive; in a few positions of each section the step is 1.6 * 4096 for every head.
All inputs are finite; a program needn't handle non-finite values. No bound on the sum of `advantage_mask` on one device may be relied on, other than what follows from the above.
Results may differ from a plain program's by a relative error of at most 0.0095.
Values may be sent and summed in bfloat16 or wider, within the bound.
A program may use at most 128 MiB of HBM per device.

v0:
```python
import jax
import jax.numpy as jnp
from jax import lax
from jax.sharding import PartitionSpec as P

STATE = 128
BLOCK = 256


def from_behind(value, axis, steps):
    count = lax.axis_size(axis)
    initial, last = (max(0, -steps), min(count, count - steps))
    return lax.ppermute(value, axis, [(source, source + steps) for source in range(initial, last)])


def swapped(block, axis, distance):
    count = lax.axis_size(axis)
    route = []
    for low in range(count):
        high = low | 1 << distance
        if high != low and high < count:
            route += [(low, high), (high, low)]
    return lax.ppermute(block, axis, route)


def mix(form, left, right):
    return jnp.einsum(form, left, right, preferred_element_type=jnp.float32)


def block_factors(seg, prev, steps_here, rate):
    cum = jnp.cumsum(-steps_here * rate[None, :], axis=0)
    enter = jnp.exp(cum) * (seg == prev)[:, None].astype(jnp.float32)
    leave = jnp.exp(cum[-1][None, :] - cum) * (seg == seg[-1])[:, None].astype(jnp.float32)
    through = jnp.exp(cum[-1]) * (seg[-1] == prev).astype(jnp.float32)
    return (cum, enter, leave, through)


def block_kernel(seg, cum):
    length = seg.shape[0]
    row = lax.broadcasted_iota(jnp.int32, (length, length), 0)
    col = lax.broadcasted_iota(jnp.int32, (length, length), 1)
    link = (seg[:, None] == seg[None, :]) & (row >= col)
    heads_first = jnp.transpose(cum)
    spread = heads_first[:, :, None] - heads_first[:, None, :]
    return jnp.exp(jnp.where(link[None, :, :], spread, -1e30))


def piece_backward(
    grad, inputs, bmat, cmat, steps_here, seg_here, first_prev, rate, skip, carry_fn
):
    tokens = grad.shape[0]
    heads = rate.shape[0]
    head_dim = grad.shape[1] // heads
    blocks = tokens // BLOCK
    grads = grad.reshape(blocks, BLOCK, heads, head_dim)
    inputs4 = inputs.reshape(blocks, BLOCK, heads, head_dim)
    bmats = bmat.reshape(blocks, BLOCK, STATE)
    cmats = cmat.reshape(blocks, BLOCK, STATE)
    segs = seg_here.reshape(blocks, BLOCK)
    prevs = jnp.concatenate([jnp.reshape(first_prev, (1,)), segs[:-1, -1]])
    step_blocks = steps_here.reshape(blocks, BLOCK, heads)
    items = (segs, prevs, step_blocks, grads, inputs4, bmats, cmats)

    def first_pass(item):
        seg, prev, steps_block, grad3, inputs3, bmat2, cmat2 = item
        cum, enter, leave, through = block_factors(seg, prev, steps_block, rate)
        xo = (leave[:, :, None] * inputs3).astype(jnp.bfloat16)
        gi = (enter[:, :, None] * grad3).astype(jnp.bfloat16)
        state = mix("tkp,tn->kpn", xo, bmat2)
        adjoint = mix("tkp,tn->kpn", gi, cmat2)
        return (through, state, adjoint, xo, gi)

    through, states, adjoints, xos, gis = lax.map(first_pass, items)
    zeros = jnp.zeros((heads, head_dim, STATE), jnp.float32)
    ones = jnp.ones((heads,), jnp.float32)

    def forward(carry, item):
        total, factor = carry
        return ((total * item[0][:, None, None] + item[1], factor * item[0]), (total, factor))

    def backward(carry, item):
        total, factor = carry
        return ((item[1] + item[0][:, None, None] * total, factor * item[0]), (total, factor))

    (fwd_total, fwd_factor), (local_in, factor_in) = lax.scan(
        forward, (zeros, ones), (through, states)
    )
    (bwd_total, discarded_result), (local_out, exiting_multiplier) = lax.scan(
        backward, (zeros, ones), (through, adjoints), reverse=True
    )
    earlier, after = carry_fn(fwd_total, fwd_factor, bwd_total)
    entering_state = (local_in + factor_in[:, :, None, None] * earlier[None]).astype(jnp.bfloat16)
    later = (local_out + exiting_multiplier[:, :, None, None] * after[None]).astype(jnp.bfloat16)

    def second_pass(item):
        seg, prev, steps_block, grad3, inputs3, bmat2, cmat2, xo, gi, enter_state, later_state = (
            item
        )
        cum, enter, leave, unused_through = block_factors(seg, prev, steps_block, rate)
        kernel = block_kernel(seg, cum)
        prod = mix("tkp,ukp->ktu", grad3, inputs3)
        w_one = (prod * kernel).astype(jnp.bfloat16)
        cross = mix("tn,un->tu", bmat2, cmat2)
        w_two = (jnp.swapaxes(kernel, 1, 2) * cross[None, :, :]).astype(jnp.bfloat16)
        grad_c = mix("ktu,un->tn", w_one, bmat2) + mix("tkp,kpn->tn", gi, enter_state)
        grad_b = mix("kut,un->tn", w_one, cmat2) + mix("tkp,kpn->tn", xo, later_state)
        grad_x = mix("ktu,ukp->tkp", w_two, grad3) + leave[:, :, None] * mix(
            "tn,kpn->tkp", bmat2, later_state
        )
        grad_x = grad_x + skip[None, :, None] * grad3.astype(jnp.float32)
        return (grad_x, grad_b, grad_c)

    grad_x, grad_b, grad_c = lax.map(second_pass, items + (xos, gis, entering_state, later))
    return (
        grad_x.reshape(tokens, heads * head_dim),
        grad_b.reshape(tokens, STATE),
        grad_c.reshape(tokens, STATE),
    )


def butterfly(buffer, send):
    slots = buffer.shape[0]
    place = lax.axis_index("seq")
    level = 0
    while 1 << level < slots:
        mine = place >> level & 1
        view = buffer.reshape((slots >> level + 1, 2, 1 << level) + buffer.shape[1:])
        half = lax.dynamic_index_in_dim(view, 1 - mine, 1, keepdims=False)
        received = send(half, level)
        view = lax.dynamic_update_index_in_dim(view, jnp.expand_dims(received, 1), 1 - mine, 1)
        buffer = view.reshape(buffer.shape)
        level += 1
    return buffer


def sweep(value, decays, piece, direction, pieces, send):
    value = send(value, direction)
    reach = 1
    while reach < pieces - 1:
        factor = jnp.ones((decays.shape[1],), jnp.float32)
        for offset in range(reach):
            index = piece - direction * (1 + offset)
            inside = (index >= 0) & (index < pieces)
            picked = lax.dynamic_index_in_dim(
                decays, jnp.clip(index, 0, pieces - 1), 0, keepdims=False
            )
            factor = factor * jnp.where(inside, picked, 1.0)
        value = value + factor[:, None, None] * send(value, direction * reach)
        reach = reach * 2
    return value


def on_device(
    previous,
    saved_head_inputs,
    input_b,
    input_c,
    steps,
    decay_rate,
    skip_gain,
    segment_ids,
    advantage_mask,
):
    section = lax.axis_index("pipe")
    arrived = from_behind(previous, "pipe", -1)
    masked = previous * advantage_mask.astype(jnp.bfloat16)[None, :, None]
    incoming = jnp.where(section == lax.axis_size("pipe") - 1, masked, arrived)[0]
    length = incoming.shape[0]
    heads = decay_rate.shape[1]
    head_dim = incoming.shape[1] // heads
    groups = input_b.shape[2] // STATE
    members = heads // groups
    devices = lax.axis_size("seq")
    place = lax.axis_index("seq")
    grad3 = incoming.reshape(length, heads, head_dim)
    inputs3 = saved_head_inputs[0].reshape(length, heads, head_dim)
    skip_part = mix("thp,thp->h", grad3, inputs3)
    bypass_gain_adjoint = lax.psum(skip_part, "seq")
    seg_all = lax.all_gather(segment_ids[0], "seq", axis=0, tiled=True)
    width = members * head_dim
    bundle = jnp.concatenate(
        [
            incoming.reshape(length, groups, width),
            saved_head_inputs[0].reshape(length, groups, width),
            input_b[0].reshape(length, groups, STATE),
            input_c[0].reshape(length, groups, STATE),
        ],
        axis=2,
    )
    bundle = jnp.swapaxes(bundle, 0, 1)

    def send_pieces(half, level):
        return swapped(half, "seq", level)

    def send_steps(half, level):
        return swapped(half.astype(jnp.bfloat16), "seq", level).astype(half.dtype)

    def send_results(half, level):
        return swapped(half, "seq", level)

    gathered_values = butterfly(bundle, send_pieces).reshape(groups * length, 2 * width + 2 * STATE)
    grad_piece = gathered_values[:, :width]
    inputs_piece = gathered_values[:, width : 2 * width]
    b_piece = gathered_values[:, 2 * width : 2 * width + STATE]
    c_piece = gathered_values[:, 2 * width + STATE :]
    step_slots = jnp.swapaxes(steps[0].reshape(length, groups, members), 0, 1)
    steps_piece = butterfly(step_slots, send_steps).reshape(groups * length, members)
    group = place % groups
    piece = place // groups
    span = groups * length
    pieces = devices // groups
    seg_piece = lax.dynamic_slice_in_dim(seg_all, piece * span, span)
    before = lax.dynamic_index_in_dim(seg_all, jnp.maximum(piece * span - 1, 0), 0, keepdims=False)
    first_prev = jnp.where(piece > 0, before, -1)
    rate = lax.dynamic_slice_in_dim(decay_rate[0], group * members, members)
    skip = lax.dynamic_slice_in_dim(skip_gain[0], group * members, members)

    def send_state(value, distance):
        return from_behind(value.astype(jnp.bfloat16), "seq", distance * groups).astype(value.dtype)

    def carry_across(total, factor, adjoint_total):
        table = lax.all_gather(factor, "seq", axis=0, tiled=True).reshape(pieces, groups, members)
        decays = lax.dynamic_index_in_dim(table, group, 1, keepdims=False)
        earlier = sweep(total, decays, piece, 1, pieces, send_state)
        after = sweep(adjoint_total, decays, piece, -1, pieces, send_state)
        return (earlier, after)

    grad_x_p, grad_b_p, grad_c_p = piece_backward(
        grad_piece,
        inputs_piece,
        b_piece,
        c_piece,
        steps_piece,
        seg_piece,
        first_prev,
        rate,
        skip,
        carry_across,
    )
    results = jnp.concatenate(
        [
            grad_x_p.astype(jnp.bfloat16),
            grad_b_p.astype(jnp.bfloat16),
            grad_c_p.astype(jnp.bfloat16),
        ],
        axis=1,
    )
    results = results.reshape(groups, length, width + 2 * STATE)
    returned = jnp.swapaxes(butterfly(results, send_results), 0, 1)
    grad_x_out = returned[:, :, :width].reshape(1, length, heads * head_dim)
    grad_b_out = returned[:, :, width : width + STATE].reshape(1, length, groups * STATE)
    grad_c_out = returned[:, :, width + STATE :].reshape(1, length, groups * STATE)
    return (grad_x_out, grad_b_out, grad_c_out, bypass_gain_adjoint.reshape(1, heads))


def solution(mesh):
    return jax.shard_map(
        on_device,
        mesh=mesh,
        in_specs=(
            P("pipe", "seq", None),
            P("pipe", "seq", None),
            P("pipe", "seq", None),
            P("pipe", "seq", None),
            P("pipe", "seq", None),
            P("pipe", None),
            P("pipe", None),
            P("pipe", "seq"),
            P("seq"),
        ),
        out_specs=(
            P("pipe", "seq", None),
            P("pipe", "seq", None),
            P("pipe", "seq", None),
            P("pipe", None),
        ),
        check_vma=False,
    )
```

profile of v0, /device:TPU:1, one launch (start us, length us, event | category | flops | bytes accessed | tf_op | source)
XLA Modules:
  0.0 565.4 jit_solution(219756111911728704)
XLA Ops:
  0.7 4.1 copy.89
  4.8 3.3 copy.90
  8.4 2.1 broadcast_multiply_fusion
  11.9 2.3 maximum_bitcast_fusion
  14.2 6.8 %copy.93 = bf16[8,128,2304]{2,1,0:T(8,128)(2,1)} copy(bf16[8,128,2304]{1,2,0:T(8,128)(2,1)} %maximum_bitcast_fusion) | data formatting | bytes 9437184 | tf_op jit(solution)/shard_map/transpose | solution.py:190
  21.0 3.3 dynamic-slice_bitcast_fusion.2
  24.3 4.7 collective-permute-done
  30.5 3.3 dynamic-slice_bitcast_fusion.1
  33.8 2.3 collective-permute-start.1
  36.1 51.4 %collective-permute-done.1 = bf16[2,2,128,2304]{3,2,1,0:T(8,128)(2,1)S(1)} collective-permute-done((bf16[2,2,128,2304]{3,2,1,0:T(8,128)(2,1)}, bf16[2,2,128,2304]{3,2,1,0:T(8,128)(2,1)S(1)}, u32[]{:S(2)}, u32[]{:S(2)}) %collective-permute-start.1) | collective-permute-done | bytes 2359328 | tf_op jit(solution)/shard_map/ppermute | solution.py:23
  89.2 3.3 dynamic-slice_bitcast_fusion
  95.4 40.7 %all-gather = s32[1,4096]{1,0:T(1,128)S(1)} all-gather(s32[1,128]{1,0:T(1,128)S(1)} %copy-done.21), channel_id=2, replica_groups=mesh['pipe'=1,'seq'=32] {'seq'}, dimensions={1}, use_global_device_ids=true | all-gather | bytes 16896 | tf_op jit(solution)/shard_map/all_gather | solution.py:179
  137.8 2.9 collective-permute-done.4
  140.9 4.1 collective-permute-done.5
  145.1 3.2 bitcast_dynamic-update-slice_fusion.3
  148.4 4.0 fusion.92
  154.1 6.4 %reshape.344 = bf16[4,256,16,64]{3,2,1,0:T(8,128)(2,1)} reshape(bf16[1024,1024]{1,0:T(8,128)(2,1)} %get-tuple-element.654) | data formatting | bytes 4194304 | tf_op jit(solution)/shard_map/reshape | solution.py:56
  160.5 5.8 %copy.104 = bf16[4,256,16,64]{1,3,2,0:T(8,128)(2,1)} copy(bf16[4,256,16,64]{3,2,1,0:T(8,128)(2,1)} %reshape.344) | data formatting | bytes 4194304 | tf_op jit(solution)/shard_map/while | solution.py:73
  166.3 4.0 reshape.339
  170.3 4.8 copy.108
  178.4 45.4 %while.70 = (s32[]{:T(128)}, f32[4,16]{1,0:T(4,128)S(1)}, f32[4,16,64,128]{3,2,1,0:T(8,128)}, f32[4,16,64,128]{3,2,1,0:T(8,128)}, bf16[4,256,16,64]{1,3,2,0:T(8,...) while((s32[]{:T(128)}, f32[4,16]{1,0:T(4,128)S(1)}, ...), condition=%wide.region_3.4_spmd, body=%wide.region_0.3_spmd.sunk | while | flops 137913408 | bytes 4549431 | solution.py:73
  183.2 2.3 fusion.139
  185.5 1.9 fusion.138
  187.5 2.1 fusion.137
  194.6 2.3 fusion.139
  196.9 1.9 fusion.138
  198.8 2.1 fusion.137
  205.9 2.3 fusion.139
  208.2 1.9 fusion.138
  210.1 2.1 fusion.137
  217.2 2.3 fusion.139
  219.5 2.0 fusion.138
  221.5 2.1 fusion.137
  225.4 8.3 %while.73 = (s32[]{:T(128)}, f32[16,64,128]{2,1,0:T(8,128)S(1)}, f32[16]{0:T(128)S(1)}, f32[4,16,64,128]{3,2,1,0:T(8,128)}, f32[4,16]{1,0:T(4,128)S(1)}, /*index...) while((s32[]{:T(128)}, f32[16,64,128]{2,1,0:T(8,128)S(1)}, ...), condition=%wide.region_5.6_spmd.clone, body=%wide.region_4.5_spmd.clone.sunk | while | flops 524323 | bytes 2622581 | solution.py:85
  234.4 2.9 collective-permute-start.9
  238.9 8.3 %while.72 = (s32[]{:T(128)}, f32[16,64,128]{2,1,0:T(8,128)S(1)}, f32[16]{0:T(128)S(1)}, f32[4,16,64,128]{3,2,1,0:T(8,128)}, f32[4,16]{1,0:T(4,128)S(1)}, /*index...) while((s32[]{:T(128)}, f32[16,64,128]{2,1,0:T(8,128)S(1)}, ...), condition=%wide.region_7.8_spmd.clone, body=%wide.region_6.7_spmd.clone.sunk | while | flops 524324 | bytes 2622093 | solution.py:88
  249.3 4.0 collective-permute-start.10
  253.3 3.3 fusion.74
  256.8 41.9 %all-reduce.1 = (f32[512]{0:T(512)S(1)}, f32[1,128]{1,0:T(1,128)}) all-reduce(f32[512]{0:T(512)S(1)} %dynamic-update-slice, f32[1,128]{1,0:T(1,128)S(1)} %bitcast.405), channel_id=1, replica_groups=mesh['pipe'=1,'seq'=32] {'seq'}, use_global_device_ids=true, to_apply=%add | all-reduce | flops 640 | bytes 5120
  301.1 4.4 collective-permute-start.11
  305.5 1.8 collective-permute-done.7
  311.8 12.0 %collective-permute-done.8 = bf16[16,64,128]{2,1,0:T(8,128)(2,1)S(1)} collective-permute-done((bf16[16,64,128]{2,1,0:T(8,128)(2,1)S(1)}, bf16[16,64,128]{2,1,0:T(8,128)(2,1)S(1)}, u32[]{:S(2)}, u32[]{:S(2)}) %collective-permute-start.8) | collective-permute-done | bytes 262176 | tf_op jit(solution)/shard_map/ppermute | solution.py:13
  325.4 58.1 %while.71 = (s32[]{:T(128)}, bf16[4,256,16,64]{1,3,2,0:T(8,128)(2,1)}, bf16[4,256,128]{2,1,0:T(8,128)(2,1)}, bf16[4,256,128]{2,1,0:T(8,128)(2,1)}, bf16[4,256,16...) while((s32[]{:T(128)}, ...), condition=%wide.region_12.13_spmd, body=%wide.region_8.12_spmd.sunk | while | flops 532828736 | bytes 14336141 | solution.py:113
  330.1 2.1 fusion.160
  332.2 2.6 convert_reduce_fusion.2
  344.7 2.1 fusion.160
  346.7 2.6 convert_reduce_fusion.2
  359.2 2.1 fusion.160
  361.3 2.6 convert_reduce_fusion.2
  373.7 2.1 fusion.160
  375.8 2.6 convert_reduce_fusion.2
  383.5 4.0 convert_element_type.207
  388.0 16.9 %pad_maximum_fusion = bf16[4,2,1,128,1280]{3,1,4,0,2:T(2,128)(2,1)S(1)} fusion(bf16[4,2,1,128,128]{3,1,4,0,2:T(2,128)(2,1)S(1)} %copy.112, bf16[4,2,1,128,128]{3,1,4,0,2:T(2,128)(2,1)S(1)} %copy.111, bf16[4,2,1,128,1024]{3,1,4,0,2:T(2,128)(2,1)} %convert_element_type.207), kind=kLoop, calls=%fused_computation.120 | loop fusion | flops 2621440 | bytes 5242880 | tf_op jit(solution)/shard_map/concatenate | solution.py:240
  404.8 4.1 constant_dynamic-slice_fusion.7
  408.9 6.1 %copy.113 = bf16[4,1,1,128,1280]{4,3,0,2,1:T(8,128)(2,1)} copy(bf16[4,1,1,128,1280]{3,1,4,0,2:T(2,128)(2,1)} %constant_dynamic-slice_fusion.7) | data formatting | bytes 2621440 | tf_op jit(solution)/shard_map/jit(dynamic_index_in_dim)/dynamic_slice | solution.py:128
  415.5 3.0 collective-permute-done.12
  418.5 6.3 %copy.114 = bf16[4,1,1,128,1280]{3,1,4,0,2:T(2,128)(2,1)} copy(bf16[4,1,1,128,1280]{4,3,0,2,1:T(8,128)(2,1)} %bitcast.79) | data formatting | bytes 2621440 | tf_op jit(solution)/shard_map/broadcast_in_dim | solution.py:130
  424.8 65.0 %dynamic_update_slice.95 = bf16[4,2,1,128,1280]{3,1,4,0,2:T(2,128)(2,1)S(1)} dynamic-update-slice(bf16[4,2,1,128,1280]{3,1,4,0,2:T(2,128)(2,1)S(1)} %pad_maximum_fusion, bf16[4,1,1,128,1280]{3,1,4,0,2:T(2,128)(2,1)} %copy.114, s32[]{:T(128)} %constant.320.clone.1, s32[]{:T(128)S(6)} %select_n.154, s32[]{:T(128)} %constant.320.clone.1, s32[]{:T(128)} %constant.320.clone.1, s32[]{:T(128)} %constant.320.clone.1) | dynamic-update-slice | bytes 2621444 | tf_op jit(solution)/shard_map/jit(dynamic_update_index_in_dim)/dynamic_update_slice | solution.py:130
  491.6 4.3 copy.115
  496.2 4.7 copy.116
  500.9 25.2 %collective-permute-done.13 = bf16[2,2,128,1280]{3,2,1,0:T(8,128)(2,1)} collective-permute-done((bf16[2,2,128,1280]{3,2,1,0:T(8,128)(2,1)}, bf16[2,2,128,1280]{3,2,1,0:T(8,128)(2,1)}, u32[]{:S(2)}, u32[]{:S(2)}) %collective-permute-start.13) | collective-permute-done | bytes 1310752 | tf_op jit(solution)/shard_map/ppermute | solution.py:23
  526.1 2.5 bitcast_dynamic-update-slice_fusion.6
  531.2 28.2 %collective-permute-done.14 = bf16[1,4,128,1280]{3,2,1,0:T(8,128)(2,1)S(1)} collective-permute-done((bf16[1,4,128,1280]{3,2,1,0:T(8,128)(2,1)S(1)}, bf16[1,4,128,1280]{3,2,1,0:T(8,128)(2,1)S(1)}, u32[]{:S(2)}, u32[]{:S(2)}) %collective-permute-start.14) | collective-permute-done | bytes 1310752 | tf_op jit(solution)/shard_map/ppermute | solution.py:23
  561.1 2.3 reshape.311
  (322 shorter events, 107.8 us)
Async XLA Ops:
  0.6 140.2 %copy-start = (f32[1,128]{1,0:T(1,128)S(1)}, f32[1,128]{1,0:T(1,128)}, u32[]{:S(2)}) copy-start(f32[1,128]{1,0:T(1,128)} %param.22) | copy-start | bytes 1540
  0.7 4.1 copy-start.22
  4.7 3.3 copy-start.12
  4.8 3.5 copy-start.13
  8.1 2.5 copy-start.2
  10.5 1.3 copy-start.3
  24.3 4.7 collective-permute-start
  33.8 53.8 %collective-permute-start.1 = (bf16[2,2,128,2304]{3,2,1,0:T(8,128)(2,1)}, bf16[2,2,128,2304]{3,2,1,0:T(8,128)(2,1)S(1)}, u32[]{:S(2)}, u32[]{:S(2)}) collective-permute-start(bf16[2,2,128,2304]{3,2,1,0:T(8,128)(2,1)} %dynamic-slice_bitcast_fusion.1), channel_id=1, source_target_pairs={{0,2},{2,0},{1,3},{3,1},{4,6},{6,4},{5,7},{7,5},{8,10},{10,8},{9,1... | collective-permute-start | bytes 7077896 | tf_op jit(solution)/shard_map/ppermute | solution.py:23
  89.1 4.5 copy-start.20
  89.2 6.3 %copy-start.21 = (s32[1,128]{1,0:T(1,128)S(1)}, s32[1,128]{1,0:T(1,128)}, u32[]{:S(2)}) copy-start(s32[1,128]{1,0:T(1,128)} %param.24) | copy-start | bytes 1540
  92.5 52.7 %collective-permute-start.2 = (bf16[1,4,128,2304]{3,2,1,0:T(8,128)(2,1)}, bf16[1,4,128,2304]{3,2,1,0:T(8,128)(2,1)}, u32[]{:S(2)}, u32[]{:S(2)}) collective-permute-start(bf16[1,4,128,2304]{3,2,1,0:T(8,128)(2,1)} %dynamic-slice_bitcast_fusion), channel_id=1, source_target_pairs={{0,4},{4,0},{1,5},{5,1},{2,6},{6,2},{3,7},{7,3},{8,12},{12,8},{9,1... | collective-permute-start | bytes 7077896 | tf_op jit(solution)/shard_map/ppermute | solution.py:23
  93.8 43.8 %collective-permute-start.3 = (bf16[4,1,128,16]{2,3,0,1:T(8,128)(2,1)S(1)}, bf16[4,1,128,16]{2,3,0,1:T(8,128)(2,1)S(1)}, u32[]{:S(2)}, u32[]{:S(2)}) collective-permute-start(bf16[4,1,128,16]{2,3,0,1:T(8,128)(2,1)S(1)} %fusion.78), channel_id=1, source_target_pairs={{0,1},{1,0},{2,3},{3,2},{4,5},{5,4},{6,7},{7,6},{8,9},{9,8},{10,11... | collective-permute-start | bytes 49160 | tf_op jit(solution)/shard_map/ppermute | solution.py:23
  137.6 3.1 collective-permute-start.4
  140.7 4.3 collective-permute-start.5
  234.4 14.9 %collective-permute-start.9 = (bf16[16,64,128]{2,1,0:T(8,128)(2,1)}, bf16[16,64,128]{2,1,0:T(8,128)(2,1)S(1)}, u32[]{:S(2)}, u32[]{:S(2)}) collective-permute-start(bf16[16,64,128]{2,1,0:T(8,128)(2,1)} %convert_element_type.200), channel_id=1, source_target_pairs={{0,8},{1,9},{2,10},{3,11},{4,12},{5,13},{6,14},{7,15},{8,16},{9,17... | collective-permute-start | bytes 786440 | tf_op jit(solution)/shard_map/ppermute | solution.py:13
  248.0 50.9 %collective-permute-start.6 = (bf16[16,64,128]{2,1,0:T(8,128)(2,1)}, bf16[16,64,128]{2,1,0:T(8,128)(2,1)S(1)}, u32[]{:S(2)}, u32[]{:S(2)}) collective-permute-start(bf16[16,64,128]{2,1,0:T(8,128)(2,1)} %convert_element_type.194), channel_id=1, source_target_pairs={{8,0},{9,1},{10,2},{11,3},{12,4},{13,5},{14,6},{15,7},{16,8},{17,9... | collective-permute-start | bytes 786440 | tf_op jit(solution)/shard_map/ppermute | solution.py:13
  249.3 50.9 %collective-permute-start.10 = (bf16[16,64,128]{2,1,0:T(8,128)(2,1)S(1)}, bf16[16,64,128]{2,1,0:T(8,128)(2,1)S(1)}, u32[]{:S(2)}, u32[]{:S(2)}) collective-permute-start(bf16[16,64,128]{2,1,0:T(8,128)(2,1)S(1)} %collective-permute-done.9), channel_id=1, source_target_pairs={{0,8},{1,9},{2,10},{3,11},{4,12},{5,13},{6,14},{7,15},{8,16},{9,17... | collective-permute-start | bytes 786440 | tf_op jit(solution)/shard_map/ppermute | solution.py:13
  253.3 52.2 %copy-start.23 = (f32[1,128]{1,0:T(1,128)S(1)}, f32[1,128]{1,0:T(1,128)}, u32[]{:S(2)}) copy-start(f32[1,128]{1,0:T(1,128)} %param.23) | copy-start | bytes 1540
  298.9 8.4 %collective-permute-start.7 = (bf16[16,64,128]{2,1,0:T(8,128)(2,1)S(1)}, bf16[16,64,128]{2,1,0:T(8,128)(2,1)S(1)}, u32[]{:S(2)}, u32[]{:S(2)}) collective-permute-start(bf16[16,64,128]{2,1,0:T(8,128)(2,1)S(1)} %collective-permute-done.6), channel_id=1, source_target_pairs={{8,0},{9,1},{10,2},{11,3},{12,4},{13,5},{14,6},{15,7},{16,8},{17,9... | collective-permute-start | bytes 786440 | tf_op jit(solution)/shard_map/ppermute | solution.py:13
  300.2 9.0 %copy-start.7 = (bf16[16,64,128]{2,1,0:T(8,128)(2,1)}, bf16[16,64,128]{2,1,0:T(8,128)(2,1)S(1)}, u32[]{:S(2)}) copy-start(bf16[16,64,128]{2,1,0:T(8,128)(2,1)S(1)} %collective-permute-done.10) | copy-start | bytes 786436
  301.1 8.1 %collective-permute-start.11 = (bf16[16,64,128]{2,1,0:T(8,128)(2,1)}, bf16[16,64,128]{2,1,0:T(8,128)(2,1)}, u32[]{:S(2)}, u32[]{:S(2)}) collective-permute-start(bf16[16,64,128]{2,1,0:T(8,128)(2,1)} %fusion.76), channel_id=1, source_target_pairs={{0,16},{1,17},{2,18},{3,19},{4,20},{5,21},{6,22},{7,23},{8,24},{9,... | collective-permute-start | bytes 786440 | tf_op jit(solution)/shard_map/ppermute | solution.py:13
  305.5 5.0 copy-start.5
  307.3 1.9 copy-start.8
  307.5 16.3 %collective-permute-start.8 = (bf16[16,64,128]{2,1,0:T(8,128)(2,1)S(1)}, bf16[16,64,128]{2,1,0:T(8,128)(2,1)S(1)}, u32[]{:S(2)}, u32[]{:S(2)}) collective-permute-start(bf16[16,64,128]{2,1,0:T(8,128)(2,1)S(1)} %fusion.75), channel_id=1, source_target_pairs={{16,0},{17,1},{18,2},{19,3},{20,4},{21,5},{22,6},{23,7},{24,8},{25... | collective-permute-start | bytes 786440 | tf_op jit(solution)/shard_map/ppermute | solution.py:13
  310.5 13.3 %copy-start.9 = (bf16[16,64,128]{2,1,0:T(8,128)(2,1)S(1)}, bf16[16,64,128]{2,1,0:T(8,128)(2,1)}, u32[]{:S(2)}) copy-start(bf16[16,64,128]{2,1,0:T(8,128)(2,1)} %copy-done.8) | copy-start | bytes 786436
  310.5 13.6 %copy-start.6 = (f32[4,16,64,128]{3,2,1,0:T(8,128)S(1)}, f32[4,16,64,128]{3,2,1,0:T(8,128)}, u32[]{:S(2)}) copy-start(f32[4,16,64,128]{3,2,1,0:T(8,128)} %get-tuple-element.349) | copy-start | bytes 6291460
  325.4 2.0 copy-start.10
  332.2 4.2 copy-start.14
  334.9 4.2 copy-start.17
  334.9 5.1 copy-start.11
  337.5 1.8 copy-start.15
  339.2 0.7 copy-start.18
  340.0 2.0 copy-start.10
  346.7 4.2 copy-start.14
  349.4 4.2 copy-start.17
  349.4 5.1 copy-start.11
  352.0 1.8 copy-start.15
  353.8 0.7 copy-start.18
  354.5 2.0 copy-start.10
  361.3 4.2 copy-start.14
  363.9 4.2 copy-start.17
  363.9 5.1 copy-start.11
  366.5 1.8 copy-start.15
  368.3 0.7 copy-start.18
  369.0 2.0 copy-start.10
  375.8 4.2 copy-start.14
  378.4 4.2 copy-start.17
  378.4 5.1 copy-start.11
  381.1 1.8 copy-start.15
  382.8 0.7 copy-start.18
  383.5 4.0 copy-start.16
  383.5 4.2 copy-start.19
  415.0 3.5 collective-permute-start.12
  495.9 30.3 %collective-permute-start.13 = (bf16[2,2,128,1280]{3,2,1,0:T(8,128)(2,1)}, bf16[2,2,128,1280]{3,2,1,0:T(8,128)(2,1)}, u32[]{:S(2)}, u32[]{:S(2)}) collective-permute-start(bf16[2,2,128,1280]{3,2,1,0:T(8,128)(2,1)} %bitcast.388), channel_id=1, source_target_pairs={{0,2},{2,0},{1,3},{3,1},{4,6},{6,4},{5,7},{7,5},{8,10},{10,8},{9,1... | collective-permute-start | bytes 3932168 | tf_op jit(solution)/shard_map/ppermute | solution.py:23
  528.6 30.7 %copy-start.4 = (bf16[2,2,2,128,1280]{4,3,2,1,0:T(8,128)(2,1)S(1)}, bf16[2,2,2,128,1280]{4,3,2,1,0:T(8,128)(2,1)}, u32[]{:S(2)}) copy-start(bf16[2,2,2,128,1280]{4,3,2,1,0:T(8,128)(2,1)} %bitcast_dynamic-update-slice_fusion.6) | copy-start | bytes 7864324
  530.2 29.2 %collective-permute-start.14 = (bf16[1,4,128,1280]{3,2,1,0:T(8,128)(2,1)S(1)}, bf16[1,4,128,1280]{3,2,1,0:T(8,128)(2,1)S(1)}, u32[]{:S(2)}, u32[]{:S(2)}) collective-permute-start(bf16[1,4,128,1280]{3,2,1,0:T(8,128)(2,1)S(1)} %dynamic-slice_bitcast_fusion.3), channel_id=1, source_target_pairs={{0,4},{4,0},{1,5},{5,1},{2,6},{6,2},{3,7},{7,3},{8,12},{12,8},{9,1... | collective-permute-start | bytes 3932168 | tf_op jit(solution)/shard_map/ppermute | solution.py:23
  561.1 4.4 copy-start.1
where the time goes:
time: 574 us; the launch traced here: 565 us
  local copies, waits for them, and re-layouts  186 us (32%)
  waiting for transfers between devices  134 us (23%)
  blocking collectives  82.6 us (14%)
  other arithmetic  72 us (13%)
  matrix products  61 us (11%)
  starting transfers between devices  22.3 us (4%)
    ppermute x9, waiting for transfers between devices, swapped(): return lax.ppermute(block, axis, route)  120 us
    dynamic_update_slice x6, local copies, waits for them, and re-layouts, butterfly(): lax.dynamic_update_index_in_dim(view, jnp.expand_dims(received, 1), 1 - m...  74 us
    dot_general x40, matrix products, mix(): return jnp.einsum(form, left, right, preferred_element_type=jnp.float32)  61 us
    unnamed x1, blocking collectives  41.9 us
    all_gather x1, blocking collectives, on_device(): seg_all = lax.all_gather(segment_ids[0], 'seq', axis=0, tiled=True)  40.7 us
    concatenate x1, other arithmetic, on_device(): jnp.concatenate([grad_x_p.astype(jnp.bfloat16), grad_b_p.astype(jnp.bfloa...  16.9 us
    dynamic_slice x4, local copies, waits for them, and re-layouts, butterfly(): half = lax.dynamic_index_in_dim(view, 1 - mine, 1, keepdims=False)  16.2 us
    dynamic_update_slice x12, other arithmetic, piece_backward(): through, states, adjoints, xos, gis = lax.map(first_pass, items)  16 us
  transfers between devices with their start and end apart: 15, of which 10 were waited for; matrix products, arithmetic and copies ran while one was open for 4% of the time, Pallas kernels for 0%

commit v1 on v0

v1 whole, which is shorter than its diff:
```python
import functools

import jax
import jax.numpy as jnp
from jax import lax
from jax.experimental import pallas as pl
from jax.experimental.pallas import tpu as pltpu
from jax.sharding import PartitionSpec as P

STATE = 128
F32 = jnp.float32
BF16 = jnp.bfloat16
NT = (((1,), (1,)), ((), ()))
TN = (((0,), (0,)), ((), ()))


def dot(left, right, dims=(((1,), (0,)), ((), ()))):
    return lax.dot_general(left, right, dims, preferred_element_type=F32)


def spread_heads(factor, group, members, head_dim):
    heads = factor.shape[1]
    width = members * head_dim
    row = lax.broadcasted_iota(jnp.int32, (heads, width), 0)
    col = lax.broadcasted_iota(jnp.int32, (heads, width), 1)
    pick = (row == group * members + col // head_dim).astype(F32).astype(BF16)
    high = factor.astype(BF16)
    low = (factor - high.astype(F32)).astype(BF16)
    return dot(high, pick) + dot(low, pick)


def states_kernel(members, head_dim, prev, xin, bmat, cmat, leave, enter, mask, state, adjoint, skip_part):
    group = pl.program_id(0)
    grad = prev[...].astype(F32) * mask[...]
    x = xin[...].astype(F32)
    skip_part[0] = jnp.sum(grad * x, axis=0, keepdims=True)
    xo = (spread_heads(leave[...], group, members, head_dim) * x).astype(BF16)
    gi = (spread_heads(enter[...], group, members, head_dim) * grad).astype(BF16)
    state[0] = dot(bmat[...], xo, TN).astype(BF16)
    adjoint[0] = dot(cmat[...], gi, TN).astype(BF16)


def local_kernel(
    members, head_dim, prev, xin, bmat, cmat, cum, cum_rows, seg_col, seg_row, mask, grad_x, grad_b, grad_c
):
    length = prev.shape[0]
    row = lax.broadcasted_iota(jnp.int32, (length, length), 0)
    col = lax.broadcasted_iota(jnp.int32, (length, length), 1)
    link = (seg_col[...] == seg_row[...]) & (col >= row)
    bias = jnp.where(link, 0.0, -1e30).astype(F32)
    b = bmat[...]
    c = cmat[...]
    cross = dot(b, c, NT)
    grad = (prev[...].astype(F32) * mask[...]).astype(BF16)
    cums = cum[0]
    total = jnp.zeros((length, length), F32)
    for head in range(members):
        lanes = slice(head * head_dim, (head + 1) * head_dim)
        g = grad[:, lanes]
        x = xin[:, lanes]
        decay = jnp.exp(jnp.where(link, cum_rows[head : head + 1, :] - cums[:, head : head + 1], bias))
        total = total + decay * dot(x, g, NT)
        grad_x[:, lanes] = dot((decay * cross).astype(BF16), g)
    total = total.astype(BF16)
    grad_b[...] = dot(total, c)
    grad_c[...] = dot(total, b, TN)


def final_kernel(
    members, head_dim, prev, xin, bmat, leave, enter, mask, skip, near_x, near_b, near_c, entering, later,
    grad_x, grad_b, grad_c
):
    group = pl.program_id(0)
    grad = prev[...].astype(F32) * mask[...]
    x = xin[...].astype(F32)
    left = spread_heads(leave[...], group, members, head_dim)
    xo = (left * x).astype(BF16)
    gi = (spread_heads(enter[...], group, members, head_dim) * grad).astype(BF16)
    after = later[0]
    grad_x[...] = (near_x[...] + left * dot(bmat[...], after) + skip[...] * grad).astype(BF16)
    grad_b[...] = (near_b[...] + dot(xo, after, NT)).astype(BF16)
    grad_c[...] = (near_c[...] + dot(gi, entering[0], NT)).astype(BF16)


def shifted(value, steps):
    count = lax.axis_size("seq")
    initial, last = (max(0, -steps), min(count, count - steps))
    return lax.ppermute(value, "seq", [(s, s + steps) for s in range(initial, last)])


def swapped(value, level):
    count = lax.axis_size("seq")
    return lax.ppermute(value, "seq", [(s, s ^ 1 << level) for s in range(count)])


def on_device(
    previous, saved_head_inputs, input_b, input_c, steps, decay_rate, skip_gain, segment_ids, advantage_mask
):
    mask = advantage_mask.astype(F32)
    source = previous[0]
    sections = lax.axis_size("pipe")
    if sections > 1:
        last = lax.axis_index("pipe") == sections - 1
        arrived = lax.ppermute(previous, "pipe", [(s, s - 1) for s in range(1, sections)])[0]
        source = jnp.where(last, source, arrived)
        mask = jnp.where(last, mask, 1.0)
    mask = mask[:, None]
    x, bmat, cmat = saved_head_inputs[0], input_b[0], input_c[0]
    length = source.shape[0]
    heads = decay_rate.shape[1]
    head_dim = source.shape[1] // heads
    groups = bmat.shape[1] // STATE
    members = heads // groups
    width = members * head_dim
    devices = lax.axis_size("seq")
    place = lax.axis_index("seq")
    seg = segment_ids[0]

    lower = jnp.tril(jnp.ones((length, length), F32))
    cum = jnp.dot(lower, -steps[0] * decay_rate, precision=lax.Precision.HIGHEST)
    enter = jnp.exp(cum) * (seg == seg[0])[:, None]
    leave = jnp.exp(cum[-1:] - cum) * (seg == seg[-1])[:, None]

    token_wide = pl.BlockSpec((length, width), lambda g: (0, g))
    token_state = pl.BlockSpec((length, STATE), lambda g: (0, g))
    factor = pl.BlockSpec((length, heads), lambda g: (0, 0))
    column = pl.BlockSpec((length, 1), lambda g: (0, 0))
    slot = pl.BlockSpec((1, STATE, width), lambda g: (g, 0, 0))
    params = pltpu.CompilerParams(dimension_semantics=("arbitrary",), vmem_limit_bytes=60 << 20)

    state, adjoint, skip_part = pl.pallas_call(
        functools.partial(states_kernel, members, head_dim),
        grid=(groups,),
        in_specs=[token_wide, token_wide, token_state, token_state, factor, factor, column],
        out_specs=[slot, slot, pl.BlockSpec((1, 1, width), lambda g: (g, 0, 0))],
        out_shape=[
            jax.ShapeDtypeStruct((groups, STATE, width), BF16),
            jax.ShapeDtypeStruct((groups, STATE, width), BF16),
            jax.ShapeDtypeStruct((groups, 1, width), F32),
        ],
        compiler_params=params,
        name="block_states",
    )(source, x, bmat, cmat, leave, enter, mask)

    near_x, near_b, near_c = pl.pallas_call(
        functools.partial(local_kernel, members, head_dim),
        grid=(groups,),
        in_specs=[
            token_wide, token_wide, token_state, token_state,
            pl.BlockSpec((1, length, members), lambda g: (g, 0, 0)),
            pl.BlockSpec((members, length), lambda g: (g, 0)),
            column,
            pl.BlockSpec((1, length), lambda g: (0, 0)),
            column,
        ],
        out_specs=[token_wide, token_state, token_state],
        out_shape=[
            jax.ShapeDtypeStruct((length, heads * head_dim), F32),
            jax.ShapeDtypeStruct((length, groups * STATE), F32),
            jax.ShapeDtypeStruct((length, groups * STATE), F32),
        ],
        compiler_params=params,
        name="within_block",
    )(
        source, x, bmat, cmat,
        jnp.swapaxes(cum.reshape(length, groups, members), 0, 1), cum.T, seg[:, None], seg[None, :], mask,
    )

    skip_sum = jnp.sum(skip_part.reshape(heads, head_dim), axis=1)
    ends = jnp.pad(jnp.stack([seg[0], seg[-1]]).astype(F32), (0, heads - 2))
    table = lax.all_gather(jnp.stack([cum[-1], ends]), "seq", axis=0)
    bypass_gain_adjoint = lax.psum(skip_sum, "seq")
    first, final = table[:, 1, 0], table[:, 1, 1]
    behind = jnp.concatenate([jnp.full((1,), -1.0, F32), final[:-1]])
    links = (first == behind).astype(F32)
    through = jnp.exp(table[:, 0]) * (links * (first == final))[:, None]
    own_link = lax.dynamic_index_in_dim(links, place, 0, keepdims=False)

    levels = groups.bit_length() - 1
    pieces = devices // groups
    rows = []
    for level in range(levels):
        spans = jnp.prod(through.reshape(devices >> level, 1 << level, heads), axis=1)
        low = (place >> level) & ~1
        rows.append(lax.dynamic_slice_in_dim(spans, low, 2, 0))
    per_piece = jnp.prod(through.reshape(pieces, groups, heads), axis=1)
    padded = jnp.pad(per_piece, ((pieces, pieces), (0, 0)), constant_values=1.0)
    rows.append(lax.dynamic_slice_in_dim(padded, place // groups, 2 * pieces + 1, 0))
    rows = jnp.concatenate(rows, axis=0)
    rows = jnp.repeat(rows, head_dim, axis=1).reshape(-1, groups, 1, width)

    fwd = state
    bwd = (adjoint.astype(F32) * own_link).astype(BF16)
    kept = []
    for level in range(levels):
        half = fwd.shape[0] // 2
        right = (place >> level & 1) == 1
        mine = jnp.where(right, half, 0)

        def keep(value):
            return lax.dynamic_slice_in_dim(value, mine, half, 0)

        def give(value):
            return lax.dynamic_slice_in_dim(value, half - mine, half, 0)

        fwd_other = swapped(give(fwd), level)
        bwd_other = swapped(give(bwd), level)
        fwd_own, bwd_own = keep(fwd), keep(bwd)
        rows = lax.dynamic_slice_in_dim(rows, mine, half, 1)
        decay_left, decay_right = rows[2 * level], rows[2 * level + 1]
        fwd_left = jnp.where(right, fwd_other, fwd_own)
        fwd_right = jnp.where(right, fwd_own, fwd_other)
        bwd_left = jnp.where(right, bwd_other, bwd_own)
        bwd_right = jnp.where(right, bwd_own, bwd_other)
        kept.append((right, mine, half, fwd_left, bwd_right, decay_left, decay_right))
        fwd = (fwd_right.astype(F32) + decay_right * fwd_left.astype(F32)).astype(BF16)
        bwd = (bwd_left.astype(F32) + decay_left * bwd_right.astype(F32)).astype(BF16)

    across = rows[2 * levels :]
    entering = jnp.zeros(fwd.shape, F32)
    later = jnp.zeros(bwd.shape, F32)
    factor_in = factor_out = jnp.ones(across.shape[1:], F32)
    for distance in range(1, pieces):
        entering = entering + factor_in * shifted(fwd, distance * groups).astype(F32)
        later = later + factor_out * shifted(bwd, -distance * groups).astype(F32)
        factor_in = factor_in * across[pieces - distance]
        factor_out = factor_out * across[pieces + distance]

    for level in reversed(range(levels)):
        right, mine, half, fwd_left, bwd_right, decay_left, decay_right = kept[level]
        in_right = (fwd_left.astype(F32) + decay_left * entering).astype(BF16)
        out_left = (bwd_right.astype(F32) + decay_right * later).astype(BF16)
        in_left, out_right = entering.astype(BF16), later.astype(BF16)
        got_in = swapped(jnp.where(right, in_left, in_right), level)
        got_out = swapped(jnp.where(right, out_left, out_right), level)
        own_in = jnp.where(right, in_right, in_left)
        own_out = jnp.where(right, out_right, out_left)

        def join(own, got):
            return jnp.concatenate([jnp.where(right, got, own), jnp.where(right, own, got)], axis=0)

        entering = join(own_in, got_in)
        later = join(own_out, got_out)
        if level:
            entering, later = entering.astype(F32), later.astype(F32)

    grad_x, grad_b, grad_c = pl.pallas_call(
        functools.partial(final_kernel, members, head_dim),
        grid=(groups,),
        in_specs=[
            token_wide, token_wide, token_state, factor, factor, column,
            pl.BlockSpec((1, width), lambda g: (0, g)),
            token_wide, token_state, token_state, slot, slot,
        ],
        out_specs=[token_wide, token_state, token_state],
        out_shape=[
            jax.ShapeDtypeStruct((length, heads * head_dim), BF16),
            jax.ShapeDtypeStruct((length, groups * STATE), BF16),
            jax.ShapeDtypeStruct((length, groups * STATE), BF16),
        ],
        compiler_params=params,
        name="across_blocks",
    )(
        source, x, bmat, leave, enter * own_link, mask, jnp.repeat(skip_gain, head_dim, axis=1),
        near_x, near_b, near_c, entering, later,
    )
    return grad_x[None], grad_b[None], grad_c[None], bypass_gain_adjoint[None]


def solution(mesh):
    return jax.shard_map(
        on_device,
        mesh=mesh,
        in_specs=(
            P("pipe", "seq", None),
            P("pipe", "seq", None),
            P("pipe", "seq", None),
            P("pipe", "seq", None),
            P("pipe", "seq", None),
            P("pipe", None),
            P("pipe", None),
            P("pipe", "seq"),
            P("seq"),
        ),
        out_specs=(
            P("pipe", "seq", None),
            P("pipe", "seq", None),
            P("pipe", "seq", None),
            P("pipe", None),
        ),
        check_vma=False,
    )
```

time: 574 us -> 243 us (0.42)
  local copies, waits for them, and re-layouts: 186 us -> 19.9 us
  waiting for transfers between devices: 134 us -> 54.1 us
  matrix products: 61 us -> 1.05 us
  other arithmetic: 72 us -> 31.1 us
  Pallas kernels: 0 us -> 29.9 us
  starting transfers between devices: 22.3 us -> 16 us
    ppermute x15 -> x18, waiting for transfers between devices: 134 us -> 54.1 us  [the longest x12 36.5 us: swapped(): lax.ppermute(value, 'seq', [(s, s ^ 1 << level) for s in range(count)])]
    dynamic_update_slice x22 -> x0, local copies, waits for them, and re-layouts: 74.8 us -> none  [the longest x6 74 us: butterfly(): lax.dynamic_update_index_in_dim(view, jnp.expand_dims(received, 1), 1 - m...]
    dot_general x40 -> x1, matrix products: 61 us -> 1.05 us  [on_device(): jnp.dot(lower, -steps[0] * decay_rate, precision=lax.Precision.HIGHEST)]
    psum x0 -> x1, blocking collectives: none -> 42.7 us  [on_device(): bypass_gain_adjoint = lax.psum(skip_sum, 'seq')]
    unnamed x1 -> x0, blocking collectives: 41.9 us -> none
    pallas_call x0 -> x3, Pallas kernels: none -> 29.9 us  [the longest x1 11 us: on_device(): pl.pallas_call(functools.partial(local_kernel, members, head_dim), grid=(...]
    dynamic_update_slice x15 -> x0, other arithmetic: 16.1 us -> none  [the longest x12 16 us: piece_backward(): through, states, adjoints, xos, gis = lax.map(first_pass, items)]
    select_n x0 -> x16, other arithmetic: none -> 15.1 us  [the longest x6 7.51 us: join(): jnp.where(right, got, own)]
  transfers between devices with their start and end apart: 15 -> 18, of which waited for: 10 -> 9; matrix products, arithmetic and copies ran while one was open for 4% -> 14% of each run, Pallas kernels for 0% -> 5%
where the time goes in v1:
time: 243 us; the launch traced here: 239 us
  blocking collectives  85.9 us (35%)
  waiting for transfers between devices  54.1 us (22%)
  other arithmetic  31.1 us (13%)
  Pallas kernels  29.9 us (12%)
  local copies, waits for them, and re-layouts  19.9 us (8%)
  starting transfers between devices  16 us (7%)
    all_gather x1, blocking collectives, on_device(): table = lax.all_gather(jnp.stack([cum[-1], ends]), 'seq', axis=0)  43.2 us
    psum x1, blocking collectives, on_device(): bypass_gain_adjoint = lax.psum(skip_sum, 'seq')  42.7 us
    ppermute x12, waiting for transfers between devices, swapped(): lax.ppermute(value, 'seq', [(s, s ^ 1 << level) for s in range(count)])  36.5 us
    ppermute x6, waiting for transfers between devices, shifted(): lax.ppermute(value, 'seq', [(s, s + steps) for s in range(initial, last)])  17.6 us
    pallas_call x1, Pallas kernels, on_device(): pl.pallas_call(functools.partial(local_kernel, members, head_dim), grid=(...  11 us
    pallas_call x1, Pallas kernels, on_device(): pl.pallas_call(functools.partial(final_kernel, members, head_dim), grid=(...  10.3 us
    pallas_call x1, Pallas kernels, on_device(): pl.pallas_call(functools.partial(states_kernel, members, head_dim), grid=...  8.55 us
    ppermute x12, starting transfers between devices, swapped(): lax.ppermute(value, 'seq', [(s, s ^ 1 << level) for s in range(count)])  8.03 us
  transfers between devices with their start and end apart: 18, of which 9 were waited for; matrix products, arithmetic and copies ran while one was open for 14% of the time, Pallas kernels for 5%

profile of v1, /device:TPU:1, one launch (start us, length us, event | category | flops | bytes accessed | tf_op | source)
XLA Modules:
  0.0 239.3 jit_solution(7071406040078290511)
XLA Ops:
  0.6 1.3 fusion.51
  1.9 1.4 add_convert_fusion
  3.3 1.0 fusion.28
  4.4 43.2 %all-gather.1 = f32[32,2,128]{2,1,0:T(2,128)S(1)} all-gather(f32[1,2,128]{2,1,0:T(2,128)S(1)} %maximum_bitcast_fusion), channel_id=2, replica_groups=mesh['pipe'=1,'seq'=32] {'seq'}, dimensions={0}, use_global_device_ids=true | all-gather | bytes 33792 | tf_op jit(solution)/shard_map/all_gather | solution.py:171
  47.6 0.5 slice_reduce_fusion.2
  48.1 0.6 slice_reduce_fusion
  48.7 0.7 convert_bitcast_fusion
  49.3 0.7 copy.31.mask
  50.1 1.9 fusion.37
  52.1 0.6 dynamic_slice.71
  52.7 1.4 broadcast_multiply_fusion
  54.1 8.5 %block_states.1 = (bf16[8,128,1024]{2,1,0:T(8,128)(2,1)}, bf16[8,128,1024]{2,1,0:T(8,128)(2,1)}, f32[8,1,1024]{2,1,0:T(1,128)}) custom-call(bf16[128,8192]{1,0:T(8,128)(2,1)} %bitcast.59, bf16[128,8192]{1,0:T(8,128)(2,1)} %bitcast.62, bf16[128,1024]{1,0:T(8,128)(2,1)} %bitcast.65, bf16[128,1024]{1,0:T(8,128)(2,1)} %bitcast.69, ...), custom_call_target="tpu_custom_call" | custom-call | tf_op jit(solution)/shard_map/block_states/pallas_call | solution.py:131
  62.6 2.4 %constant_dynamic-slice_fusion.14 = bf16[4,128,1024]{2,1,0:T(8,128)(2,1)} fusion(bf16[8,128,1024]{2,1,0:T(8,128)(2,1)} %get-tuple-element.16, s32[]{:T(128)S(6)} %select_n.224), kind=kLoop, calls=%fused_computation.111 | loop fusion | bytes 2097156 | tf_op jit(solution)/shard_map/dynamic_slice | solution.py:204
  65.2 1.2 multiply_convert_fusion
  66.4 1.0 constant_dynamic-slice_fusion.7
  67.4 0.4 collective-permute-start.9
  69.3 1.3 broadcast_in_dim.38
  70.6 2.3 reshape_reshape.3
  72.8 0.8 dynamic-slice_bitcast_fusion.1
  73.6 2.0 fusion.1
  75.7 0.9 constant_dynamic-slice_fusion.10
  76.8 0.5 fusion.4
  77.3 1.0 copy-done
  78.3 0.8 constant_dynamic-slice_fusion.6
  79.1 1.2 collective-permute-start.10
  80.3 0.9 dynamic-slice_bitcast_fusion.3
  81.2 9.0 %collective-permute-done.1 = bf16[2,128,1024]{2,1,0:T(8,128)(2,1)} collective-permute-done((bf16[2,128,1024]{2,1,0:T(8,128)(2,1)}, bf16[2,128,1024]{2,1,0:T(8,128)(2,1)}, u32[]{:S(2)}, u32[]{:S(2)}) %collective-permute-start.1) | collective-permute-done | bytes 524320 | tf_op jit(solution)/shard_map/ppermute | solution.py:93
  90.2 1.4 fusion.11
  91.8 9.7 %collective-permute-done.10 = bf16[2,128,1024]{2,1,0:T(8,128)(2,1)} collective-permute-done((bf16[2,128,1024]{2,1,0:T(8,128)(2,1)}, bf16[2,128,1024]{2,1,0:T(8,128)(2,1)}, u32[]{:S(2)}, u32[]{:S(2)}) %collective-permute-start.10) | collective-permute-done | bytes 524320 | tf_op jit(solution)/shard_map/ppermute | solution.py:93
  101.4 1.3 fusion.14
  102.8 0.9 constant_dynamic-slice_fusion.8
  103.9 1.3 collective-permute-start.5
  105.2 1.3 collective-permute-start.4
  106.5 1.3 collective-permute-start.3
  107.8 1.8 collective-permute-done.11
  109.8 1.3 collective-permute-start.14
  111.1 1.3 collective-permute-start.13
  112.4 1.5 collective-permute-start.12
  113.9 1.9 collective-permute-done.4
  115.8 5.6 %collective-permute-done.3 = bf16[1,128,1024]{2,1,0:T(8,128)(2,1)S(1)} collective-permute-done((bf16[1,128,1024]{2,1,0:T(8,128)(2,1)S(1)}, bf16[1,128,1024]{2,1,0:T(8,128)(2,1)S(1)}, u32[]{:S(2)}, u32[]{:S(2)}) %collective-permute-start.3) | collective-permute-done | bytes 262176 | tf_op jit(solution)/shard_map/ppermute | solution.py:88
  121.7 1.2 collective-permute-start.6
  122.9 10.1 %collective-permute-done.13 = bf16[1,128,1024]{2,1,0:T(8,128)(2,1)S(1)} collective-permute-done((bf16[1,128,1024]{2,1,0:T(8,128)(2,1)S(1)}, bf16[1,128,1024]{2,1,0:T(8,128)(2,1)S(1)}, u32[]{:S(2)}, u32[]{:S(2)}) %collective-permute-start.13) | collective-permute-done | bytes 262176 | tf_op jit(solution)/shard_map/ppermute | solution.py:88
  133.3 0.4 collective-permute-start.15
  134.0 1.7 collective-permute-start.7
  135.7 5.0 %collective-permute-done.15 = bf16[1,128,1024]{2,1,0:T(8,128)(2,1)S(1)} collective-permute-done((bf16[1,128,1024]{2,1,0:T(8,128)(2,1)S(1)}, bf16[1,128,1024]{2,1,0:T(8,128)(2,1)S(1)}, u32[]{:S(2)}, u32[]{:S(2)}) %collective-permute-start.15) | collective-permute-done | bytes 262176 | tf_op jit(solution)/shard_map/ppermute | solution.py:93
  140.7 1.3 fusion.17
  142.1 4.8 %collective-permute-done.7 = bf16[2,128,1024]{2,1,0:T(8,128)(2,1)S(1)} collective-permute-done((bf16[2,128,1024]{2,1,0:T(8,128)(2,1)S(1)}, bf16[2,128,1024]{2,1,0:T(8,128)(2,1)S(1)}, u32[]{:S(2)}, u32[]{:S(2)}) %collective-permute-start.7) | collective-permute-done | bytes 524320 | tf_op jit(solution)/shard_map/ppermute | solution.py:93
  147.0 0.4 broadcast_select_fusion.10
  147.5 3.3 %fusion.9 = bf16[4,128,1024]{2,1,0:T(8,128)(2,1)} fusion(f32[4,1024]{1,0:T(4,128)S(1)} %get-tuple-element.51, pred[]{:T(512)S(6)} %eq.68, bf16[2,128,1024]{2,1,0:T(8,128)(2,1)S(1)} %broadcast_select_fusion.9, bf16[2,128,1024]{2,1,0:T(8,128)(2,1)S(1)} %get-tuple-element.33, bf16[4,128,1024]{2,1,0:T(8,128)(2,1)} %collective-permute-done, ...), kind=kLoop, calls=%fused_computation.16 | loop fusion | flops 4194304 | bytes 4210693 | tf_op jit(solution)/shard_map/jit(_where)/select_n | solution.py:234
  150.8 1.3 collective-permute-start.8
  152.1 6.1 %collective-permute-done.16 = bf16[2,128,1024]{2,1,0:T(8,128)(2,1)S(1)} collective-permute-done((bf16[2,128,1024]{2,1,0:T(8,128)(2,1)S(1)}, bf16[2,128,1024]{2,1,0:T(8,128)(2,1)S(1)}, u32[]{:S(2)}, u32[]{:S(2)}) %collective-permute-start.16) | collective-permute-done | bytes 524320 | tf_op jit(solution)/shard_map/ppermute | solution.py:93
  158.2 1.5 broadcast_select_fusion.7
  159.8 1.8 fusion.7
  161.6 1.6 collective-permute-start.17
  163.4 0.7 broadcast_in_dim.37.skip
  164.1 0.7 copy.28.seg_col
  164.8 1.1 copy.26
  166.2 11.0 %within_block.1 = (f32[128,8192]{1,0:T(8,128)}, f32[128,1024]{1,0:T(8,128)}, f32[128,1024]{1,0:T(8,128)}) custom-call(bf16[128,8192]{1,0:T(8,128)(2,1)} %bitcast.60, bf16[128,8192]{1,0:T(8,128)(2,1)} %bitcast.63, bf16[128,1024]{1,0:T(8,128)(2,1)} %bitcast.66, bf16[128,1024]{1,0:T(8,128)(2,1)} %bitcast.70, f32[8,128,16]{2,1,0:T(8,128)} %bitcast.68, ...), custom_call_target="tpu_custom_call" | custom-call | tf_op jit(solution)/shard_map/within_block/pallas_call | solution.py:145
  177.2 42.7 %psum.7 = f32[1,128]{1,0:T(1,128)} all-reduce(f32[1,128]{1,0:T(1,128)S(1)} %bitcast.91), channel_id=1, replica_groups=mesh['pipe'=1,'seq'=32] {'seq'}, use_global_device_ids=true, to_apply=%region_4.5 | all-reduce | flops 128 | bytes 1024 | tf_op jit(solution)/shard_map/psum | solution.py:172
  219.9 3.2 %broadcast_select_fusion.4 = (bf16[4,128,1024]{2,1,0:T(8,128)(2,1)S(1)}, bf16[4,128,1024]{2,1,0:T(8,128)(2,1)S(1)}) fusion(bf16[4,128,1024]{2,1,0:T(8,128)(2,1)} %collective-permute-done.8, pred[]{:T(512)S(6)} %eq.68, bf16[2,128,1024]{2,1,0:T(8,128)(2,1)} %copy-done.5, bf16[2,128,1024]{2,1,0:T(8,128)(2,1)} %copy-done.8, f32[4,1024]{1,0:T(4,128)S(1)} %get-tuple-element.51, ...), kind=kLoop, calls=%fused_computation.33 | loop fusion | flops 4718592 | bytes 6307845 | tf_op jit(solution)/shard_map/jit(_where)/select_n | solution.py:240
  223.3 1.5 pad_maximum_fusion.entering
  224.8 2.3 broadcast_select_fusion.1
  227.2 1.6 pad_maximum_fusion.1.later
  228.8 10.3 %across_blocks.1 = (bf16[128,8192]{1,0:T(8,128)(2,1)}, bf16[128,1024]{1,0:T(8,128)(2,1)}, bf16[128,1024]{1,0:T(8,128)(2,1)}) custom-call(bf16[128,8192]{1,0:T(8,128)(2,1)} %bitcast.61, bf16[128,8192]{1,0:T(8,128)(2,1)} %bitcast.64, bf16[128,1024]{1,0:T(8,128)(2,1)} %bitcast.67, f32[128,128]{1,0:T(8,128)} %get-tuple-element.54.leave, ...), custom_call_target="tpu_custom_call" | custom-call | tf_op jit(solution)/shard_map/across_blocks/pallas_call | solution.py:247
  (92 shorter events, 4.3 us)
Async XLA Ops:
  62.6 2.6 %copy-start.11 = (bf16[8,128,1024]{2,1,0:T(8,128)(2,1)S(1)}, bf16[8,128,1024]{2,1,0:T(8,128)(2,1)}, u32[]{:S(2)}) copy-start(bf16[8,128,1024]{2,1,0:T(8,128)(2,1)} %get-tuple-element.17) | copy-start | bytes 6291460
  65.0 8.6 %collective-permute-start = (bf16[4,128,1024]{2,1,0:T(8,128)(2,1)}, bf16[4,128,1024]{2,1,0:T(8,128)(2,1)}, u32[]{:S(2)}, u32[]{:S(2)}) collective-permute-start(bf16[4,128,1024]{2,1,0:T(8,128)(2,1)} %constant_dynamic-slice_fusion.14), channel_id=1, source_target_pairs={{0,1},{1,0},{2,3},{3,2},{4,5},{5,4},{6,7},{7,6},{8,9},{9,8},{10,11... | collective-permute-start | bytes 3145736 | tf_op jit(solution)/shard_map/ppermute | solution.py:93
  67.4 9.1 %collective-permute-start.9 = (bf16[4,128,1024]{2,1,0:T(8,128)(2,1)}, bf16[4,128,1024]{2,1,0:T(8,128)(2,1)S(1)}, u32[]{:S(2)}, u32[]{:S(2)}) collective-permute-start(bf16[4,128,1024]{2,1,0:T(8,128)(2,1)} %constant_dynamic-slice_fusion.7), channel_id=1, source_target_pairs={{0,1},{1,0},{2,3},{3,2},{4,5},{5,4},{6,7},{7,6},{8,9},{9,8},{10,11... | collective-permute-start | bytes 3145736 | tf_op jit(solution)/shard_map/ppermute | solution.py:93
  75.7 1.1 copy-start.2
  76.6 13.6 %collective-permute-start.1 = (bf16[2,128,1024]{2,1,0:T(8,128)(2,1)}, bf16[2,128,1024]{2,1,0:T(8,128)(2,1)}, u32[]{:S(2)}, u32[]{:S(2)}) collective-permute-start(bf16[2,128,1024]{2,1,0:T(8,128)(2,1)} %constant_dynamic-slice_fusion.10), channel_id=1, source_target_pairs={{0,2},{1,3},{2,0},{3,1},{4,6},{5,7},{6,4},{7,5},{8,10},{9,11},{10,... | collective-permute-start | bytes 1572872 | tf_op jit(solution)/shard_map/ppermute | solution.py:93
  77.3 1.0 copy-start
  79.1 22.4 %collective-permute-start.10 = (bf16[2,128,1024]{2,1,0:T(8,128)(2,1)}, bf16[2,128,1024]{2,1,0:T(8,128)(2,1)}, u32[]{:S(2)}, u32[]{:S(2)}) collective-permute-start(bf16[2,128,1024]{2,1,0:T(8,128)(2,1)} %constant_dynamic-slice_fusion.6), channel_id=1, source_target_pairs={{0,2},{1,3},{2,0},{3,1},{4,6},{5,7},{6,4},{7,5},{8,10},{9,11},{10,... | collective-permute-start | bytes 1572872 | tf_op jit(solution)/shard_map/ppermute | solution.py:93
  80.3 21.1 %copy-start.1 = (bf16[4,128,1024]{2,1,0:T(8,128)(2,1)S(1)}, bf16[4,128,1024]{2,1,0:T(8,128)(2,1)}, u32[]{:S(2)}) copy-start(bf16[4,128,1024]{2,1,0:T(8,128)(2,1)} %copy-done) | copy-start | bytes 3145732
  91.7 12.0 %collective-permute-start.2 = (bf16[1,128,1024]{2,1,0:T(8,128)(2,1)S(1)}, bf16[1,128,1024]{2,1,0:T(8,128)(2,1)S(1)}, u32[]{:S(2)}, u32[]{:S(2)}) collective-permute-start(bf16[1,128,1024]{2,1,0:T(8,128)(2,1)S(1)} %constant_dynamic-slice_fusion.9), channel_id=1, source_target_pairs={{0,4},{1,5},{2,6},{3,7},{4,0},{5,1},{6,2},{7,3},{8,12},{9,13},{10,... | collective-permute-start | bytes 786440 | tf_op jit(solution)/shard_map/ppermute | solution.py:93
  102.8 6.9 %collective-permute-start.11 = (bf16[1,128,1024]{2,1,0:T(8,128)(2,1)S(1)}, bf16[1,128,1024]{2,1,0:T(8,128)(2,1)S(1)}, u32[]{:S(2)}, u32[]{:S(2)}) collective-permute-start(bf16[1,128,1024]{2,1,0:T(8,128)(2,1)S(1)} %constant_dynamic-slice_fusion.5), channel_id=1, source_target_pairs={{0,4},{1,5},{2,6},{3,7},{4,0},{5,1},{6,2},{7,3},{8,12},{9,13},{10,... | collective-permute-start | bytes 786440 | tf_op jit(solution)/shard_map/ppermute | solution.py:93
  103.9 8.5 %collective-permute-start.5 = (bf16[1,128,1024]{2,1,0:T(8,128)(2,1)S(1)}, bf16[1,128,1024]{2,1,0:T(8,128)(2,1)S(1)}, u32[]{:S(2)}, u32[]{:S(2)}) collective-permute-start(bf16[1,128,1024]{2,1,0:T(8,128)(2,1)S(1)} %fusion.21), channel_id=1, source_target_pairs={{0,24},{1,25},{2,26},{3,27},{4,28},{5,29},{6,30},{7,31}} | collective-permute-start | bytes 786440 | tf_op jit(solution)/shard_map/ppermute | solution.py:88
  105.2 10.6 %collective-permute-start.4 = (bf16[1,128,1024]{2,1,0:T(8,128)(2,1)S(1)}, bf16[1,128,1024]{2,1,0:T(8,128)(2,1)S(1)}, u32[]{:S(2)}, u32[]{:S(2)}) collective-permute-start(bf16[1,128,1024]{2,1,0:T(8,128)(2,1)S(1)} %fusion.21), channel_id=1, source_target_pairs={{0,16},{1,17},{2,18},{3,19},{4,20},{5,21},{6,22},{7,23},{8,24},{9,... | collective-permute-start | bytes 786440 | tf_op jit(solution)/shard_map/ppermute | solution.py:88
  106.5 14.9 %collective-permute-start.3 = (bf16[1,128,1024]{2,1,0:T(8,128)(2,1)S(1)}, bf16[1,128,1024]{2,1,0:T(8,128)(2,1)S(1)}, u32[]{:S(2)}, u32[]{:S(2)}) collective-permute-start(bf16[1,128,1024]{2,1,0:T(8,128)(2,1)S(1)} %fusion.21), channel_id=1, source_target_pairs={{0,8},{1,9},{2,10},{3,11},{4,12},{5,13},{6,14},{7,15},{8,16},{9,17... | collective-permute-start | bytes 786440 | tf_op jit(solution)/shard_map/ppermute | solution.py:88
  109.8 13.1 %collective-permute-start.14 = (bf16[1,128,1024]{2,1,0:T(8,128)(2,1)S(1)}, bf16[1,128,1024]{2,1,0:T(8,128)(2,1)S(1)}, u32[]{:S(2)}, u32[]{:S(2)}) collective-permute-start(bf16[1,128,1024]{2,1,0:T(8,128)(2,1)S(1)} %fusion.24), channel_id=1, source_target_pairs={{24,0},{25,1},{26,2},{27,3},{28,4},{29,5},{30,6},{31,7}} | collective-permute-start | bytes 786440 | tf_op jit(solution)/shard_map/ppermute | solution.py:88
  111.1 21.9 %collective-permute-start.13 = (bf16[1,128,1024]{2,1,0:T(8,128)(2,1)S(1)}, bf16[1,128,1024]{2,1,0:T(8,128)(2,1)S(1)}, u32[]{:S(2)}, u32[]{:S(2)}) collective-permute-start(bf16[1,128,1024]{2,1,0:T(8,128)(2,1)S(1)} %fusion.24), channel_id=1, source_target_pairs={{16,0},{17,1},{18,2},{19,3},{20,4},{21,5},{22,6},{23,7},{24,8},{25... | collective-permute-start | bytes 786440 | tf_op jit(solution)/shard_map/ppermute | solution.py:88
  112.4 20.6 %collective-permute-start.12 = (bf16[1,128,1024]{2,1,0:T(8,128)(2,1)S(1)}, bf16[1,128,1024]{2,1,0:T(8,128)(2,1)S(1)}, u32[]{:S(2)}, u32[]{:S(2)}) collective-permute-start(bf16[1,128,1024]{2,1,0:T(8,128)(2,1)S(1)} %fusion.24), channel_id=1, source_target_pairs={{8,0},{9,1},{10,2},{11,3},{12,4},{13,5},{14,6},{15,7},{16,8},{17,9... | collective-permute-start | bytes 786440 | tf_op jit(solution)/shard_map/ppermute | solution.py:88
  121.7 12.0 %copy-start.3 = (bf16[4,128,1024]{2,1,0:T(8,128)(2,1)S(1)}, bf16[4,128,1024]{2,1,0:T(8,128)(2,1)}, u32[]{:S(2)}) copy-start(bf16[4,128,1024]{2,1,0:T(8,128)(2,1)} %copy-done.2) | copy-start | bytes 3145732
  121.7 11.9 %collective-permute-start.6 = (bf16[1,128,1024]{2,1,0:T(8,128)(2,1)S(1)}, bf16[1,128,1024]{2,1,0:T(8,128)(2,1)S(1)}, u32[]{:S(2)}, u32[]{:S(2)}) collective-permute-start(bf16[1,128,1024]{2,1,0:T(8,128)(2,1)S(1)} %get-tuple-element.35), channel_id=1, source_target_pairs={{0,4},{1,5},{2,6},{3,7},{4,0},{5,1},{6,2},{7,3},{8,12},{9,13},{10,... | collective-permute-start | bytes 786440 | tf_op jit(solution)/shard_map/ppermute | solution.py:93
  133.3 7.3 %collective-permute-start.15 = (bf16[1,128,1024]{2,1,0:T(8,128)(2,1)S(1)}, bf16[1,128,1024]{2,1,0:T(8,128)(2,1)S(1)}, u32[]{:S(2)}, u32[]{:S(2)}) collective-permute-start(bf16[1,128,1024]{2,1,0:T(8,128)(2,1)S(1)} %get-tuple-element.28), channel_id=1, source_target_pairs={{0,4},{1,5},{2,6},{3,7},{4,0},{5,1},{6,2},{7,3},{8,12},{9,13},{10,... | collective-permute-start | bytes 786440 | tf_op jit(solution)/shard_map/ppermute | solution.py:93
  134.0 13.0 %collective-permute-start.7 = (bf16[2,128,1024]{2,1,0:T(8,128)(2,1)S(1)}, bf16[2,128,1024]{2,1,0:T(8,128)(2,1)S(1)}, u32[]{:S(2)}, u32[]{:S(2)}) collective-permute-start(bf16[2,128,1024]{2,1,0:T(8,128)(2,1)S(1)} %fusion.19), channel_id=1, source_target_pairs={{0,2},{1,3},{2,0},{3,1},{4,6},{5,7},{6,4},{7,5},{8,10},{9,11},{10,... | collective-permute-start | bytes 1572872 | tf_op jit(solution)/shard_map/ppermute | solution.py:93
  142.0 5.5 %copy-start.4 = (bf16[8,128,1024]{2,1,0:T(8,128)(2,1)S(1)}, bf16[8,128,1024]{2,1,0:T(8,128)(2,1)}, u32[]{:S(2)}) copy-start(bf16[8,128,1024]{2,1,0:T(8,128)(2,1)} %get-tuple-element.16) | copy-start | bytes 6291460
  142.0 16.2 %collective-permute-start.16 = (bf16[2,128,1024]{2,1,0:T(8,128)(2,1)S(1)}, bf16[2,128,1024]{2,1,0:T(8,128)(2,1)S(1)}, u32[]{:S(2)}, u32[]{:S(2)}) collective-permute-start(bf16[2,128,1024]{2,1,0:T(8,128)(2,1)S(1)} %fusion.17), channel_id=1, source_target_pairs={{0,2},{1,3},{2,0},{3,1},{4,6},{5,7},{6,4},{7,5},{8,10},{9,11},{10,... | collective-permute-start | bytes 1572872 | tf_op jit(solution)/shard_map/ppermute | solution.py:93
  147.4 3.4 %copy-start.8 = (bf16[2,128,1024]{2,1,0:T(8,128)(2,1)}, bf16[2,128,1024]{2,1,0:T(8,128)(2,1)S(1)}, u32[]{:S(2)}) copy-start(bf16[2,128,1024]{2,1,0:T(8,128)(2,1)S(1)} %get-tuple-element.33) | copy-start | bytes 1572868
  147.5 3.3 %copy-start.5 = (bf16[2,128,1024]{2,1,0:T(8,128)(2,1)}, bf16[2,128,1024]{2,1,0:T(8,128)(2,1)S(1)}, u32[]{:S(2)}) copy-start(bf16[2,128,1024]{2,1,0:T(8,128)(2,1)S(1)} %broadcast_select_fusion.9) | copy-start | bytes 1572868
  150.8 69.1 %collective-permute-start.8 = (bf16[4,128,1024]{2,1,0:T(8,128)(2,1)}, bf16[4,128,1024]{2,1,0:T(8,128)(2,1)}, u32[]{:S(2)}, u32[]{:S(2)}) collective-permute-start(bf16[4,128,1024]{2,1,0:T(8,128)(2,1)} %fusion.9), channel_id=1, source_target_pairs={{0,1},{1,0},{2,3},{3,2},{4,5},{5,4},{6,7},{7,6},{8,9},{9,8},{10,11... | collective-permute-start | bytes 3145736 | tf_op jit(solution)/shard_map/ppermute | solution.py:93
  159.7 1.9 copy-start.9
  159.8 1.8 copy-start.6
  159.8 3.5 %copy-start.15 = (f32[1,128]{1,0:T(1,128)S(1)}, f32[1,128]{1,0:T(1,128)}, u32[]{:S(2)}) copy-start(f32[1,128]{1,0:T(1,128)} %param.15) | copy-start | bytes 1540
  159.8 4.3 %copy-start.14 = (s32[1,128]{1,0:T(1,128)S(1)}, s32[1,128]{1,0:T(1,128)}, u32[]{:S(2)}) copy-start(s32[1,128]{1,0:T(1,128)} %seg_row.1) | copy-start | bytes 1540
  159.8 6.1 %copy-start.13 = (f32[8,1,1024]{2,1,0:T(1,128)S(1)}, f32[8,1,1024]{2,1,0:T(1,128)}, u32[]{:S(2)}) copy-start(f32[8,1,1024]{2,1,0:T(1,128)} %get-tuple-element.21) | copy-start | bytes 98308
  161.6 63.2 %collective-permute-start.17 = (bf16[4,128,1024]{2,1,0:T(8,128)(2,1)}, bf16[4,128,1024]{2,1,0:T(8,128)(2,1)}, u32[]{:S(2)}, u32[]{:S(2)}) collective-permute-start(bf16[4,128,1024]{2,1,0:T(8,128)(2,1)} %fusion.7), channel_id=1, source_target_pairs={{0,1},{1,0},{2,3},{3,2},{4,5},{5,4},{6,7},{7,6},{8,9},{9,8},{10,11... | collective-permute-start | bytes 3145736 | tf_op jit(solution)/shard_map/ppermute | solution.py:93
  163.3 2.9 %copy-start.12 = (f32[128,128]{0,1:T(8,128)}, f32[128,128]{0,1:T(8,128)S(1)}, u32[]{:S(2)}) copy-start(f32[128,128]{0,1:T(8,128)S(1)} %copy.25) | copy-start | bytes 196612
  223.3 1.6 copy-start.7
  223.3 1.5 copy-start.10
